TPU v7x, 512 devices: a 4x2x32 block of a 4x8x32 slice. The times are simulated.
512 devices in a mesh: grp: 2 (over y), blk: 128 (over z, x), uly: 2 (over core).
Axes of the slice: x: 4, y: 2, z: 32, core: 2. Of those that a mesh axis runs over, the one named last changes fastest.
The devices are a block of a 4x8x32 slice.
Arguments:
- query: bfloat16 [8192, 1152], P(('grp', 'blk', 'uly')), parts along dimension 0, may hold values from -6 to 6
- key: bfloat16 [8192, 1152], P(('grp', 'blk', 'uly')), parts along dimension 0, may hold values from -6 to 6
- value: bfloat16 [8192, 1152], P(('grp', 'blk', 'uly')), parts along dimension 0, may hold values from -6 to 6
- q_gain: float32 [96], replicated, may hold values from 1 to 2.5
- k_gain: float32 [96], replicated, may hold values from 1 to 2.5
- out_weight: bfloat16 [1152, 2304], P('uly'), may hold values from -0.1875 to 0.1875
Outputs:
- mixed: bfloat16 [8192, 2304], P(('grp', 'blk', 'uly')), parts along dimension 0
There are 2 independent parts, one for each index of `grp`. A program takes and returns all parts, laid end to end along the dimension named above; an argument that names none is the same for every part. Nothing has to cross between parts.
All inputs are finite; a program needn't handle non-finite values.
Results may differ from a plain program's by a relative error of at most 0.012.
Values may be sent and summed in bfloat16 or wider, within the bound.
A program may use at most 128 MiB of HBM per device.

v0:
```python
import jax
import jax.numpy as jnp
from jax import lax
from jax.sharding import Mesh
from jax.sharding import PartitionSpec as P

H = 12
HD = 96
GRP_BLK_ULY = ("grp", "blk_0", "blk_1", "uly")


def whole_of(shard, axes, dim):
    if not axes:
        return shard
    nearer = lax.all_gather(shard, axes[-1], axis=dim, tiled=True)
    return whole_of(nearer, axes[:-1], dim)


def split_up(shard, dim, length):
    dims = shard.shape
    blocks = shard.reshape(*dims[:dim], length, dims[dim] // length, *dims[dim + 1 :])
    return jnp.moveaxis(blocks, dim, 0)


def sent_and_summed(shard, axis, dim):
    length = lax.axis_size(axis)
    blocks = lax.all_to_all(split_up(shard, dim, length), axis, 0, 0, tiled=True)
    return jnp.sum(blocks.astype(jnp.float32), axis=0)


def normed(data, gain):
    tok_rows = data.shape[0]
    grid = data.astype(jnp.float32).reshape(tok_rows, H, HD)
    meansq = jnp.mean(grid * grid, axis=-1, keepdims=True)
    return (grid * lax.rsqrt(meansq + 1e-06) * gain).astype(jnp.bfloat16).reshape(tok_rows, H * HD)


def attend_block(query_heads, kv_piece):
    length = kv_piece.shape[1]
    head_count = query_heads.shape[1]
    key_heads = kv_piece[0].reshape(length, head_count, HD)
    value_heads = kv_piece[1].reshape(length, head_count, HD)
    score_scale = float(HD) ** (-0.5)
    scores = (
        jnp.einsum("qhd,khd->hqk", query_heads, key_heads, preferred_element_type=jnp.float32)
        * score_scale
    )
    expd = jnp.exp(scores)
    total_weight = jnp.sum(expd, axis=-1).T
    weighted = jnp.einsum(
        "hqk,khd->qhd", expd.astype(jnp.bfloat16), value_heads, preferred_element_type=jnp.float32
    )
    return (weighted, total_weight)


def on_device(query, key, value, q_gain, k_gain, out_weight):
    query_normed = normed(query, q_gain)
    key_normed = normed(key, k_gain)
    query_group, key_group, value_group = (
        lax.all_to_all(query_normed, "uly", split_axis=1, concat_axis=0, tiled=True),
        lax.all_to_all(key_normed, "uly", split_axis=1, concat_axis=0, tiled=True),
        lax.all_to_all(value, "uly", split_axis=1, concat_axis=0, tiled=True),
    )
    row_count = query_group.shape[0]
    local_heads = query_group.shape[1] // HD
    query_heads = query_group.reshape(row_count, local_heads, HD)
    kv_stack = jnp.stack([key_group, value_group])
    weighted, total_weight = attend_block(query_heads, whole_of(kv_stack, ("blk_1", "blk_0"), 1))
    attn = (
        (weighted / total_weight[:, :, None])
        .astype(jnp.bfloat16)
        .reshape(row_count, local_heads * HD)
    )
    mixed = sent_and_summed(
        jnp.dot(attn, out_weight, preferred_element_type=jnp.float32).astype(jnp.bfloat16), "uly", 0
    )
    return mixed.astype(jnp.bfloat16)


def solution(mesh):
    split = Mesh(
        mesh.devices.reshape(mesh.shape["grp"], 32, 4, mesh.shape["uly"]),
        ("grp", "blk_0", "blk_1", "uly"),
    )
    in_specs = (
        P(GRP_BLK_ULY, None),
        P(GRP_BLK_ULY, None),
        P(GRP_BLK_ULY, None),
        P(),
        P(),
        P("uly", None),
    )
    out_specs = P(GRP_BLK_ULY, None)
    return jax.shard_map(
        on_device, mesh=split, in_specs=in_specs, out_specs=out_specs, check_vma=False
    )
```

profile of v0, /device:TPU:33, one launch (start us, length us, event | category | flops | bytes accessed | tf_op | source)
XLA Modules:
  0.0 334.8 jit_solution(16086594618422082272)
XLA Ops:
  6.5 0.0 copy-start
  6.6 0.0 copy-start.2
  6.6 0.0 copy-start.3
  6.6 0.9 convert_multiply_fusion.3
  7.5 0.1 mul.67
  7.6 0.1 reduce_sum.39
  7.7 0.1 mul.68
  7.8 0.1 mul.69
  7.9 0.7 mul.71
  8.6 0.1 mul.72
  8.7 0.8 fusion.13
  9.5 0.1 all_to_all.39
  9.6 0.6 copy.22
  10.2 44.7 %all-to-all-start = ((bf16[16,2,576]{2,0,1:T(8,128)(2,1)}), bf16[16,2,576]{2,0,1:T(8,128)(2,1)S(1)}, u32[]{:S(2)}, u32[]{:S(2)}) async-start(bf16[16,2,576]{2,0,1:T(8,128)(2,1)} %copy.22), calls=%async_computation | async-start | bytes 81920 | tf_op jit(solution)/shard_map/all_to_all | solution.py:61
  54.9 0.0 all-gather.3.cloned.1.call-start
  54.9 0.9 all_to_all.42
  55.8 0.2 all-to-all-done
  56.0 3.8 %all_to_all.53 = bf16[16,2,576]{2,0,1:T(8,128)(2,1)S(1)} all-to-all(bf16[16,2,576]{2,0,1:T(8,128)(2,1)S(1)} %copy.23), channel_id=1, replica_groups=mesh['grp'=2,'blk_0'=32,'blk_1'=4,'uly'=2] {'uly'}, dimensions={1} | all-to-all | bytes 73728 | tf_op jit(solution)/shard_map/all_to_all | solution.py:62
  59.7 0.6 pad_maximum_fusion
  60.4 0.1 all-gather.3.cloned.1.call-update
  60.4 0.1 all-gather.5.cloned.1.call-start
  60.5 101.1 %all-gather.3.cloned.1.call-done = bf16[2,1024,576]{2,1,0:T(8,128)(2,1)} async-done(((bf16[2,32,576]{2,1,0:T(8,128)(2,1)}), bf16[2,1024,576]{2,1,0:T(8,128)(2,1)}) %all-gather.3.cloned.1.call-update) | async-done | bytes 2359312 | tf_op jit(solution)/shard_map/all_gather | solution.py:15
  161.6 0.1 all-gather.5.cloned.1.call-update
  161.7 0.8 convert_multiply_fusion.1
  162.5 0.1 mul.76
  162.6 0.1 reduce_sum.40
  162.7 0.1 mul.77
  162.8 0.1 mul.78
  162.9 0.0 copy-done.3
  162.9 0.1 mul.81
  163.0 0.0 copy-done.2
  163.0 0.1 all_to_all.45
  163.1 25.3 %all_to_all.54 = bf16[16,2,576]{2,0,1:T(8,128)(2,1)S(1)} all-to-all(bf16[16,2,576]{2,0,1:T(8,128)(2,1)S(1)} %copy.25), channel_id=1, replica_groups=mesh['grp'=2,'blk_0'=32,'blk_1'=4,'uly'=2] {'uly'}, dimensions={1} | all-to-all | bytes 73728 | tf_op jit(solution)/shard_map/all_to_all | solution.py:60
  188.5 0.1 reshape.50
  188.6 104.1 %all-gather.5.cloned.1.call-done = bf16[2,4096,576]{2,1,0:T(8,128)(2,1)} async-done(((bf16[2,1024,576]{2,1,0:T(8,128)(2,1)}), bf16[2,4096,576]{2,1,0:T(8,128)(2,1)}) %all-gather.5.cloned.1.call-update) | async-done | bytes 9437200 | tf_op jit(solution)/shard_map/all_gather | solution.py:15
  292.6 8.9 %fusion.17 = (bf16[1,4096,576]{2,1,0:T(8,128)(2,1)}, bf16[1,4096,576]{2,1,0:T(8,128)(2,1)}) fusion(bf16[2,4096,576]{2,1,0:T(8,128)(2,1)} %all-gather.5.cloned.1.call-done), kind=kLoop, calls=%fused_computation.20 | loop fusion | bytes 18874368 | tf_op jit(solution)/shard_map/slice | solution.py:41
  301.5 7.6 %copy.26 = bf16[1,4096,576]{1,2,0:T(8,128)(2,1)} copy(bf16[1,4096,576]{2,1,0:T(8,128)(2,1)} %get-tuple-element.5) | data formatting | bytes 9437184 | tf_op jit(solution)/shard_map/slice | solution.py:41
  309.2 7.6 %copy.24 = bf16[1,4096,576]{1,2,0:T(8,128)(2,1)} copy(bf16[1,4096,576]{2,1,0:T(8,128)(2,1)} %get-tuple-element.6) | data formatting | bytes 9437184 | tf_op jit(solution)/shard_map/slice | solution.py:42
  316.8 0.0 copy-start.1
  316.8 3.5 %fusion.18 = (f32[6,32]{1,0:T(8,128)S(1)}, bf16[6,32,4096]{2,1,0:T(8,128)(2,1)S(1)}) fusion(bf16[4096,6,96]{0,2,1:T(8,128)(2,1)} %bitcast.22, bf16[32,6,96]{2,1,0:T(8,128)(2,1)S(1)} %reshape.50), kind=kOutput, calls=%fused_computation.21 | convolution fusion | flops 153354048 | bytes 6329088 | tf_op jit(solution)/shard_map/qhd,khd->hqk/dot_general | solution.py:45
  320.3 0.3 copy-done.1
  320.5 1.8 fusion.9
  322.4 0.1 reshape.51
  322.5 0.0 copy-done
  322.5 0.5 convolution_convert_fusion
  323.0 4.3 %all_to_all.55 = bf16[2,16,2304]{2,1,0:T(8,128)(2,1)S(1)} all-to-all(bf16[2,16,2304]{2,1,0:T(8,128)(2,1)S(1)} %bitcast.24), channel_id=1, replica_groups=mesh['grp'=2,'blk_0'=32,'blk_1'=4,'uly'=2] {'uly'}, dimensions={0} | all-to-all | bytes 294912 | tf_op jit(solution)/shard_map/all_to_all | solution.py:27
  327.3 0.7 reduce_sum.42
  (7 shorter events, 0.1 us)
Async XLA Ops:
  6.5 315.9 %copy-start = (bf16[576,2304]{1,0:T(8,128)(2,1)S(1)}, bf16[576,2304]{1,0:T(8,128)(2,1)}, u32[]{:S(2)}) copy-start(bf16[576,2304]{1,0:T(8,128)(2,1)} %param.11) | copy-start | bytes 7962628
  6.6 156.4 %copy-start.2 = (bf16[16,1152]{1,0:T(8,128)(2,1)S(1)}, bf16[16,1152]{1,0:T(8,128)(2,1)}, u32[]{:S(2)}) copy-start(bf16[16,1152]{1,0:T(8,128)(2,1)} %param.6) | copy-start | bytes 110596
  6.6 156.3 %copy-start.3 = (f32[96]{0:T(128)S(1)}, f32[96]{0:T(128)}, u32[]{:S(2)}) copy-start(f32[96]{0:T(128)} %param.9) | copy-start | bytes 1156
  10.2 45.8 %all-to-all-start = ((bf16[16,2,576]{2,0,1:T(8,128)(2,1)}), bf16[16,2,576]{2,0,1:T(8,128)(2,1)S(1)}, u32[]{:S(2)}, u32[]{:S(2)}) async-start(bf16[16,2,576]{2,0,1:T(8,128)(2,1)} %copy.22), calls=%async_computation | async-start | bytes 81920 | tf_op jit(solution)/shard_map/all_to_all | solution.py:61
  54.9 106.7 %all-gather.3.cloned.1.call-start = ((), (), s32[]{:S(2)}) async-start(), calls=%async_computation.4 | async-start | bytes 2703360 | tf_op jit(solution)/shard_map/all_gather | solution.py:15
  60.4 232.2 %all-gather.5.cloned.1.call-start = ((), (), s32[]{:S(2)}) async-start(), calls=%async_computation.5 | async-start | bytes 13107200 | tf_op jit(solution)/shard_map/all_gather | solution.py:15
  316.8 3.8 %copy-start.1 = (bf16[1,4096,576]{1,2,0:T(8,128)(2,1)S(1)}, bf16[1,4096,576]{1,2,0:T(8,128)(2,1)}, u32[]{:S(2)}) copy-start(bf16[1,4096,576]{1,2,0:T(8,128)(2,1)} %copy.24) | copy-start | bytes 14155780
Sparse Core Ops, SparseCore 0:
  60.5 101.0 all-gather.2
  163.7 128.8 all-gather.4
where the time goes:
time: 336 us; the launch traced here: 335 us
  waiting for transfers between devices  205 us (61%)
  starting transfers between devices  44.8 us (13%)
  blocking collectives  33.4 us (10%)
  local copies, waits for them, and re-layouts  27.8 us (8%)
  between operations  13.6 us (4%)
  matrix products  5.82 us (2%)
  other arithmetic  4.04 us (1%)
    all_gather x2, waiting for transfers between devices, whole_of(): nearer = lax.all_gather(shard, axes[-1], axis=dim, tiled=True)  205 us
    all_to_all x1, starting transfers between devices, on_device(): lax.all_to_all(key_normed, 'uly', split_axis=1, concat_axis=0, tiled=True)  44.7 us
    all_to_all x1, blocking collectives, on_device(): lax.all_to_all(query_normed, 'uly', split_axis=1, concat_axis=0, tiled=True)  25.3 us
    slice x2, local copies, waits for them, and re-layouts, attend_block(): key_heads = kv_piece[0].reshape(length, head_count, HD)  16.5 us
    slice x1, local copies, waits for them, and re-layouts, attend_block(): value_heads = kv_piece[1].reshape(length, head_count, HD)  7.59 us
  transfers between devices with their start and end apart: 3, of which 3 were waited for; matrix products, arithmetic and copies ran while one was open for 0% of the time, Pallas kernels for 0%

commit v1 on v0

--- a/solution.py
+++ b/solution.py
@@ -57,7 +57,12 @@
     query_normed = normed(query, q_gain)
     key_normed = normed(key, k_gain)
     query_group, key_group, value_group = (
-        lax.all_to_all(query_normed, "uly", split_axis=1, concat_axis=0, tiled=True),
+        jnp.concatenate(
+            lax.all_to_all(
+                jnp.stack(jnp.split(query_normed, lax.axis_size("uly"), axis=1)), "uly", 0, 0
+            ),
+            axis=0,
+        ),
         lax.all_to_all(key_normed, "uly", split_axis=1, concat_axis=0, tiled=True),
         lax.all_to_all(value, "uly", split_axis=1, concat_axis=0, tiled=True),
     )

time: 336 us -> 335 us (level)
  transfers between devices with their start and end apart: 3 -> 3, of which waited for: 3 -> 2; matrix products, arithmetic and copies ran while one was open for 0% -> 1% of each run, Pallas kernels for 0% -> 0%
where the time goes in v1:
time: 335 us; the launch traced here: 334 us
  waiting for transfers between devices  205 us (61%)
  starting transfers between devices  44.8 us (13%)
  blocking collectives  33.2 us (10%)
  local copies, waits for them, and re-layouts  27.7 us (8%)
  between operations  13.6 us (4%)
  matrix products  5.82 us (2%)
  other arithmetic  3.89 us (1%)
    all_gather x2, waiting for transfers between devices, whole_of(): nearer = lax.all_gather(shard, axes[-1], axis=dim, tiled=True)  205 us
    all_to_all x1, starting transfers between devices, on_device(): lax.all_to_all(value, 'uly', split_axis=1, concat_axis=0, tiled=True)  44.7 us
    all_to_all x1, blocking collectives, on_device(): lax.all_to_all(jnp.stack(jnp.split(query_normed, lax.axis_size('uly'), ax...  25.3 us
    slice x2, local copies, waits for them, and re-layouts, attend_block(): key_heads = kv_piece[0].reshape(length, head_count, HD)  16.4 us
    slice x1, local copies, waits for them, and re-layouts, attend_block(): value_heads = kv_piece[1].reshape(length, head_count, HD)  7.66 us
  transfers between devices with their start and end apart: 3, of which 2 were waited for; matrix products, arithmetic and copies ran while one was open for 1% of the time, Pallas kernels for 0%

profile of v1, /device:TPU:33, one launch (start us, length us, event | category | flops | bytes accessed | tf_op | source)
XLA Modules:
  0.0 334.3 jit_solution(15244721206752113820)
XLA Ops:
  6.5 0.0 copy-start
  6.6 0.0 copy-start.1
  6.6 0.0 copy-start.2
  6.6 1.0 all_to_all.33
  7.6 0.6 copy.21
  8.2 44.7 %all-to-all-start.1 = ((bf16[16,2,576]{2,0,1:T(8,128)(2,1)}), bf16[16,2,576]{2,0,1:T(8,128)(2,1)S(1)}, u32[]{:S(2)}, u32[]{:S(2)}) async-start(bf16[16,2,576]{2,0,1:T(8,128)(2,1)} %copy.21), calls=%async_computation.1 | async-start | bytes 81920 | tf_op jit(solution)/shard_map/all_to_all | solution.py:67
  52.9 0.0 all-gather.3.cloned.1.call-start
  52.9 0.8 convert_multiply_fusion.3
  53.7 0.1 mul.67
  53.8 0.1 reduce_sum.39
  53.9 0.1 mul.68
  54.0 0.1 mul.69
  54.1 0.7 mul.71
  54.8 0.1 mul.72
  54.9 0.8 fusion.13
  55.7 0.1 all_to_all.30
  55.8 0.0 all-to-all-done.1
  55.8 3.5 %all_to_all.42 = bf16[16,2,576]{2,0,1:T(8,128)(2,1)S(1)} all-to-all(bf16[16,2,576]{2,0,1:T(8,128)(2,1)S(1)} %copy.20), channel_id=1, replica_groups=mesh['grp'=2,'blk_0'=32,'blk_1'=4,'uly'=2] {'uly'}, dimensions={1} | all-to-all | bytes 73728 | tf_op jit(solution)/shard_map/all_to_all | solution.py:66
  59.3 0.6 pad_maximum_fusion
  60.0 0.1 all-gather.3.cloned.1.call-update
  60.0 0.1 all-gather.5.cloned.1.call-start
  60.1 101.1 %all-gather.3.cloned.1.call-done = bf16[2,1024,576]{2,1,0:T(8,128)(2,1)} async-done(((bf16[2,32,576]{2,1,0:T(8,128)(2,1)}), bf16[2,1024,576]{2,1,0:T(8,128)(2,1)}) %all-gather.3.cloned.1.call-update) | async-done | bytes 2359312 | tf_op jit(solution)/shard_map/all_gather | solution.py:15
  161.2 0.1 all-gather.5.cloned.1.call-update
  161.3 0.8 convert_multiply_fusion.1
  162.1 0.1 mul.76
  162.2 0.1 reduce_sum.40
  162.3 0.1 mul.77
  162.4 0.1 mul.78
  162.5 0.0 copy-done.2
  162.5 0.1 mul.81
  162.6 0.0 copy-done.1
  162.6 0.1 slice_bitcast_fusion.1
  162.7 25.3 %all_to_all.43 = bf16[2,16,576]{2,1,0:T(8,128)(2,1)S(1)} all-to-all(bf16[2,16,576]{2,1,0:T(8,128)(2,1)S(1)} %pad_maximum_fusion.1), channel_id=1, replica_groups=mesh['grp'=2,'blk_0'=32,'blk_1'=4,'uly'=2] {'uly'}, dimensions={0} | all-to-all | bytes 73728 | tf_op jit(solution)/shard_map/all_to_all | solution.py:61
  188.1 0.1 reshape_reshape.3
  188.2 104.1 %all-gather.5.cloned.1.call-done = bf16[2,4096,576]{2,1,0:T(8,128)(2,1)} async-done(((bf16[2,1024,576]{2,1,0:T(8,128)(2,1)}), bf16[2,4096,576]{2,1,0:T(8,128)(2,1)}) %all-gather.5.cloned.1.call-update) | async-done | bytes 9437200 | tf_op jit(solution)/shard_map/all_gather | solution.py:15
  292.3 8.8 %fusion.17 = (bf16[1,4096,576]{2,1,0:T(8,128)(2,1)}, bf16[1,4096,576]{2,1,0:T(8,128)(2,1)}) fusion(bf16[2,4096,576]{2,1,0:T(8,128)(2,1)} %all-gather.5.cloned.1.call-done), kind=kLoop, calls=%fused_computation.23 | loop fusion | bytes 18874368 | tf_op jit(solution)/shard_map/slice | solution.py:41
  301.0 7.7 %copy.22 = bf16[1,4096,576]{1,2,0:T(8,128)(2,1)} copy(bf16[1,4096,576]{2,1,0:T(8,128)(2,1)} %get-tuple-element.6) | data formatting | bytes 9437184 | tf_op jit(solution)/shard_map/slice | solution.py:42
  308.7 0.0 slice-start
  308.7 7.7 %copy.23 = bf16[1,4096,576]{1,2,0:T(8,128)(2,1)} copy(bf16[1,4096,576]{2,1,0:T(8,128)(2,1)} %get-tuple-element.5) | data formatting | bytes 9437184 | tf_op jit(solution)/shard_map/slice | solution.py:41
  316.4 3.5 %fusion.18 = (f32[6,32]{1,0:T(8,128)S(1)}, bf16[6,32,4096]{2,1,0:T(8,128)(2,1)S(1)}) fusion(bf16[4096,6,96]{0,2,1:T(8,128)(2,1)} %bitcast.25, bf16[32,6,96]{2,1,0:T(8,128)(2,1)S(1)} %reshape_reshape.3), kind=kOutput, calls=%fused_computation.24 | convolution fusion | flops 153354048 | bytes 6329088 | tf_op jit(solution)/shard_map/qhd,khd->hqk/dot_general | solution.py:45
  319.9 0.0 slice-done
  319.9 0.1 slice-done.1
  320.0 1.8 fusion.9
  321.8 0.1 reshape.43
  321.9 0.0 copy-done
  321.9 0.5 convolution_convert_fusion
  322.5 4.3 %all_to_all.44 = bf16[2,16,2304]{2,1,0:T(8,128)(2,1)S(1)} all-to-all(bf16[2,16,2304]{2,1,0:T(8,128)(2,1)S(1)} %bitcast.29), channel_id=1, replica_groups=mesh['grp'=2,'blk_0'=32,'blk_1'=4,'uly'=2] {'uly'}, dimensions={0} | all-to-all | bytes 294912 | tf_op jit(solution)/shard_map/all_to_all | solution.py:27
  326.8 0.7 reduce_sum.42
  (9 shorter events, 0.1 us)
Async XLA Ops:
  6.5 315.4 %copy-start = (bf16[576,2304]{1,0:T(8,128)(2,1)S(1)}, bf16[576,2304]{1,0:T(8,128)(2,1)}, u32[]{:S(2)}) copy-start(bf16[576,2304]{1,0:T(8,128)(2,1)} %param.11) | copy-start | bytes 7962628
  6.6 156.1 %copy-start.1 = (bf16[16,1152]{1,0:T(8,128)(2,1)S(1)}, bf16[16,1152]{1,0:T(8,128)(2,1)}, u32[]{:S(2)}) copy-start(bf16[16,1152]{1,0:T(8,128)(2,1)} %param.6) | copy-start | bytes 110596
  6.6 156.0 %copy-start.2 = (f32[96]{0:T(128)S(1)}, f32[96]{0:T(128)}, u32[]{:S(2)}) copy-start(f32[96]{0:T(128)} %param.9) | copy-start | bytes 1156
  8.2 47.6 %all-to-all-start.1 = ((bf16[16,2,576]{2,0,1:T(8,128)(2,1)}), bf16[16,2,576]{2,0,1:T(8,128)(2,1)S(1)}, u32[]{:S(2)}, u32[]{:S(2)}) async-start(bf16[16,2,576]{2,0,1:T(8,128)(2,1)} %copy.21), calls=%async_computation.1 | async-start | bytes 81920 | tf_op jit(solution)/shard_map/all_to_all | solution.py:67
  52.9 108.3 %all-gather.3.cloned.1.call-start = ((), (), s32[]{:S(2)}) async-start(), calls=%async_computation.4 | async-start | bytes 2703360 | tf_op jit(solution)/shard_map/all_gather | solution.py:15
  60.0 232.2 %all-gather.5.cloned.1.call-start = ((), (), s32[]{:S(2)}) async-start(), calls=%async_computation.5 | async-start | bytes 13107200 | tf_op jit(solution)/shard_map/all_gather | solution.py:15
  308.7 11.2 %slice-start = ((s8[4718592]{0:T(1024)(128)(4,1)}), s8[524288]{0:T(1024)(128)(4,1)S(1)}, s32[]{:S(2)}) async-start(s8[4718592]{0:T(1024)(128)(4,1)} %bitcast.26), calls=%async_computation.6 | async-start | bytes 1048576
  316.4 3.6 %slice-start.1 = ((s8[4718592]{0:T(1024)(128)(4,1)}), s8[4194304]{0:T(1024)(128)(4,1)S(1)}, s32[]{:S(2)}) async-start(s8[4718592]{0:T(1024)(128)(4,1)} %bitcast.26), calls=%async_computation.7 | async-start | bytes 8388608
Sparse Core Ops, SparseCore 0:
  60.2 101.0 all-gather.2
  163.4 128.8 all-gather.4
